TPU v7x, 32 devices: a whole 2x2x4 slice. The times are simulated.
32 devices in a mesh: floor: 4 (over y, x), zone: 8 (over z, core).
Axes of the slice: x: 2, y: 2, z: 4, core: 2. Of those that a mesh axis runs over, the one named last changes fastest.
Arguments:
- factor: float32 [512, 96, 384], P(('floor', 'zone')), may hold values from -0.625 to 0.625
- plant_map: float32 [512, 96, 384], P(('floor', 'zone')), may hold values from -0.4082483 to 0.4082483
- offset: float32 [512, 384], P(('floor', 'zone')), may hold values from -10 to 10
- start_plan: float32 [512, 384], P(('floor', 'zone')), may hold values from -10 to 10
- demand: float32 [4, 48], replicated, may hold values from -768 to 768
- start_price: float32 [4, 48], replicated, may hold values from -6 to 6
- start_multiplier: float32 [512, 48], P(('floor', 'zone')), may hold values from -6 to 6
- neighbors: int32 [512, 4], P(('floor', 'zone')), may hold values from 0 to 127
- loop_of_zone: int32 [512], P(('floor', 'zone')), may hold values from 0 to 3
Outputs:
- control: float32 [512, 384], P(('floor', 'zone'))
- price: float32 [4, 48], replicated
- multiplier: float32 [512, 48], P(('floor', 'zone'))
Inputs may be any that keep to these rules, and one draw needn't show every extreme that they name: `neighbors`: indices count zones within the zone's own floor of 128 consecutive zones.
All inputs are finite; a program needn't handle non-finite values.
Results may differ from a plain program's by a relative error of at most 0.0001.
Values sent between devices are 32-bit elements; how exact they have to be, the bound alone decides.
No kernel may reach another device: no remote copies, remote signals or barrier semaphores. Data moves between devices by JAX's collectives and lax.ppermute only.
A program may use at most 64 MiB of HBM per device.

v0:
```python
import jax
import jax.numpy as jnp
from jax import lax
from jax.sharding import PartitionSpec as P

HORIZON = 48
NEIGHBORS = 4
LOOPS = 4
ITERS = 2


def select_rows(neighbors, count):
    columns = jnp.arange(count, dtype=jnp.int32)
    picks = (neighbors[:, :, None] == columns[None, None, :]).astype(jnp.float32)
    return jnp.sum(picks, axis=1) / NEIGHBORS


def local(
    factor,
    plant_map,
    offset,
    start_plan,
    demand,
    start_price,
    start_multiplier,
    neighbors,
    loop_of_zone,
):
    control = start_plan
    price = start_price
    multiplier = start_multiplier
    zones_here = control.shape[0]
    zones_all = zones_here * lax.axis_size("floor") * lax.axis_size("zone")
    onehot = (loop_of_zone[:, None] == jnp.arange(LOOPS, dtype=jnp.int32)[None, :]).astype(
        jnp.float32
    )
    for step in range(ITERS):
        outputs = jnp.einsum("zkv,zv->zk", plant_map, control, precision=lax.Precision.HIGHEST)
        shares = outputs[:, :HORIZON]
        bound = outputs[:, HORIZON:]
        partial_load = jnp.dot(onehot.T, shares, precision=lax.Precision.HIGHEST)
        floor_load = lax.psum(partial_load, "zone")
        total = lax.psum(floor_load, "floor")
        excess = (total - demand) * (LOOPS / zones_all)
        shift = jnp.dot(onehot, excess + price, precision=lax.Precision.HIGHEST)
        price = price + excess
        target_share = shares - shift
        floor_bound = lax.all_gather(bound, "zone", axis=0, tiled=True)
        weights = select_rows(neighbors, floor_bound.shape[0])
        near = jnp.dot(weights, floor_bound, precision=lax.Precision.HIGHEST)
        target_bound = (bound + near) / 2.0 - multiplier
        multiplier = multiplier + (bound - near) / 2.0
        target = jnp.concatenate([target_share, target_bound], axis=1)
        control = (
            0.8 * jnp.einsum("zkv,zk->zv", factor, target, precision=lax.Precision.HIGHEST) - offset
        )
    return (control, price, multiplier)


def solution(mesh):
    placed = (
        P(("floor", "zone"), None, None),
        P(("floor", "zone"), None, None),
        P(("floor", "zone"), None),
        P(("floor", "zone"), None),
        P(),
        P(),
        P(("floor", "zone"), None),
        P(("floor", "zone"), None),
        P(("floor", "zone")),
    )
    return jax.shard_map(
        local,
        mesh=mesh,
        in_specs=placed,
        out_specs=(P(("floor", "zone"), None), P(), P(("floor", "zone"), None)),
        check_vma=False,
    )
```

profile of v0, /device:TPU:0, one launch (start us, length us, event | category | flops | bytes accessed | tf_op | source)
XLA Modules:
  0.0 91.8 jit_solution(17976281189199001725)
XLA Ops:
  0.6 0.0 copy-start
  0.7 4.4 %fusion.5 = f32[16,1,96]{2,1,0:T(1,128)S(1)} fusion(f32[16,96,384]{2,1,0:T(8,128)} %param.10, f32[16,384,1]{1,0,2:T(8,128)} %bitcast.43), kind=kOutput, calls=%fused_computation.11 | convolution fusion | flops 7077888 | bytes 2390016 | tf_op jit(solution)/shard_map/zkv,zv->zk/dot_general | solution.py:38
  5.1 0.1 slice.17
  5.2 15.7 %all_gather.6 = f32[128,48]{1,0:T(8,128)S(1)} all-gather(f32[16,48]{1,0:T(8,128)S(1)} %slice.17), channel_id=1, replica_groups=mesh['floor'=4,'zone'=8] {'zone'}, dimensions={0}, use_global_device_ids=true | all-gather | bytes 27648 | tf_op jit(solution)/shard_map/all_gather | solution.py:48
  20.9 0.1 convert_reduce_fusion
  21.0 0.2 multiply_subtract_fusion.1
  21.1 0.0 copy-done.8
  21.1 0.3 fusion.8
  21.4 16.9 %psum.28 = f32[4,48]{1,0:T(4,128)S(1)} all-reduce(f32[4,48]{1,0:T(4,128)S(1)} %fusion.8), channel_id=1, replica_groups=mesh['floor'=4,'zone'=8] {'zone'}, use_global_device_ids=true, to_apply=%region_0.0 | all-reduce | flops 192 | bytes 1536 | tf_op jit(solution)/shard_map/psum | solution.py:42
  38.3 9.9 %psum.29 = f32[4,48]{1,0:T(4,128)S(1)} all-reduce(f32[4,48]{1,0:T(4,128)S(1)} %psum.28), channel_id=1, replica_groups=mesh['floor'=4,'zone'=8] {'floor'}, use_global_device_ids=true, to_apply=%region_1.0 | all-reduce | flops 192 | bytes 1536 | tf_op jit(solution)/shard_map/psum | solution.py:43
  48.2 0.2 convolution_subtract_fusion.1
  48.4 0.1 pad_maximum_fusion
  48.5 1.4 %fusion.24 = f32[16,1,384]{2,1,0:T(1,128)S(1)} fusion(f32[16,96,1]{1,2,0:T(1,128)S(1)} %bitcast.41, f32[16,96,384]{2,1,0:T(8,128)S(1)} %copy-done), kind=kOutput, calls=%fused_computation.39 | convolution fusion | flops 7077888 | bytes 2390016 | tf_op jit(solution)/shard_map/zkv,zk->zv/dot_general | solution.py:55
  49.9 2.6 %fusion.3 = f32[16,1,96]{2,1,0:T(1,128)S(1)} fusion(f32[16,96,384]{2,1,0:T(8,128)S(1)} %copy-done.1, f32[16,384,1]{1,0,2:T(8,128)S(1)} %fusion.2), kind=kOutput, calls=%fused_computation.9 | convolution fusion | flops 7077888 | bytes 2390016 | tf_op jit(solution)/shard_map/zkv,zv->zk/dot_general | solution.py:38
  52.5 0.1 slice.19
  52.6 14.0 %all_gather.7 = f32[128,48]{1,0:T(8,128)S(1)} all-gather(f32[16,48]{1,0:T(8,128)S(1)} %slice.19), channel_id=1, replica_groups=mesh['floor'=4,'zone'=8] {'zone'}, dimensions={0}, use_global_device_ids=true | all-gather | bytes 27648 | tf_op jit(solution)/shard_map/all_gather | solution.py:48
  66.6 0.8 multiply_add_fusion
  67.4 0.3 fusion.7
  67.6 13.9 %psum.30 = f32[4,48]{1,0:T(4,128)S(1)} all-reduce(f32[4,48]{1,0:T(4,128)S(1)} %fusion.7), channel_id=1, replica_groups=mesh['floor'=4,'zone'=8] {'zone'}, use_global_device_ids=true, to_apply=%region_3.0 | all-reduce | flops 192 | bytes 1536 | tf_op jit(solution)/shard_map/psum | solution.py:42
  81.5 7.9 %psum.31 = f32[4,48]{1,0:T(4,128)S(1)} all-reduce(f32[4,48]{1,0:T(4,128)S(1)} %psum.30), channel_id=1, replica_groups=mesh['floor'=4,'zone'=8] {'floor'}, use_global_device_ids=true, to_apply=%region_4.0 | all-reduce | flops 192 | bytes 1536 | tf_op jit(solution)/shard_map/psum | solution.py:43
  89.5 0.2 convolution_subtract_fusion
  89.7 0.1 pad_maximum_fusion.1
  89.8 1.4 %fusion.25 = f32[16,1,384]{2,1,0:T(1,128)S(1)} fusion(f32[16,96,1]{1,2,0:T(1,128)S(1)} %bitcast.42, f32[16,96,384]{2,1,0:T(8,128)S(1)} %copy-done), kind=kOutput, calls=%fused_computation.40 | convolution fusion | flops 7077888 | bytes 2390016 | tf_op jit(solution)/shard_map/zkv,zk->zv/dot_general | solution.py:55
  91.2 0.6 fusion
  (18 shorter events, 0.1 us)
Async XLA Ops:
  0.6 47.8 %copy-start = (f32[16,96,384]{2,1,0:T(8,128)S(1)}, f32[16,96,384]{2,1,0:T(8,128)}, u32[]{:S(2)}) copy-start(f32[16,96,384]{2,1,0:T(8,128)} %param.9) | copy-start | bytes 7077892
  0.6 20.3 %copy-start.3 = (f32[16,48]{1,0:T(8,128)S(1)}, f32[16,48]{1,0:T(8,128)}, u32[]{:S(2)}) copy-start(f32[16,48]{1,0:T(8,128)} %param.15) | copy-start | bytes 9220
  0.7 20.2 %copy-start.4 = (s32[16,4]{0,1:T(4,128)S(1)}, s32[16,4]{0,1:T(4,128)}, u32[]{:S(2)}) copy-start(s32[16,4]{0,1:T(4,128)} %param.16) | copy-start | bytes 772
  0.7 20.5 %copy-start.8 = (s32[16]{0:T(128)S(1)}, s32[16]{0:T(128)}, u32[]{:S(2)}) copy-start(s32[16]{0:T(128)} %param.17) | copy-start | bytes 196
  0.7 47.5 %copy-start.5 = (f32[4,48]{1,0:T(4,128)S(1)}, f32[4,48]{1,0:T(4,128)}, u32[]{:S(2)}) copy-start(f32[4,48]{1,0:T(4,128)} %param.14) | copy-start | bytes 2308
  0.7 47.5 %copy-start.6 = (f32[4,48]{1,0:T(4,128)S(1)}, f32[4,48]{1,0:T(4,128)}, u32[]{:S(2)}) copy-start(f32[4,48]{1,0:T(4,128)} %param.13) | copy-start | bytes 2308
  0.7 49.2 %copy-start.2 = (f32[16,384]{1,0:T(8,128)S(1)}, f32[16,384]{1,0:T(8,128)}, u32[]{:S(2)}) copy-start(f32[16,384]{1,0:T(8,128)} %param.11) | copy-start | bytes 73732
  48.2 1.7 %copy-start.1 = (f32[16,96,384]{2,1,0:T(8,128)S(1)}, f32[16,96,384]{2,1,0:T(8,128)}, u32[]{:S(2)}) copy-start(f32[16,96,384]{2,1,0:T(8,128)} %param.10) | copy-start | bytes 7077892
  89.5 2.3 %copy-start.7 = (f32[4,48]{1,0:T(4,128)}, f32[4,48]{1,0:T(4,128)S(1)}, u32[]{:S(2)}) copy-start(f32[4,48]{1,0:T(4,128)S(1)} %multiply_add_fusion.2) | copy-start | bytes 2308
where the time goes:
time: 92.1 us; the launch traced here: 91.8 us
  blocking collectives  78.3 us (85%)
  matrix products  11.7 us (13%)
    psum x2, blocking collectives, local(): floor_load = lax.psum(partial_load, 'zone')  30.8 us
    all_gather x2, blocking collectives, local(): floor_bound = lax.all_gather(bound, 'zone', axis=0, tiled=True)  29.7 us
    psum x2, blocking collectives, local(): total = lax.psum(floor_load, 'floor')  17.8 us
    dot_general x2, matrix products, local(): jnp.einsum('zkv,zv->zk', plant_map, control, precision=lax.Precision.HIGH...  7 us
    dot_general x2, matrix products, local(): jnp.einsum('zkv,zk->zv', factor, target, precision=lax.Precision.HIGHEST)  2.88 us

commit v1 on v0

--- a/solution.py
+++ b/solution.py
@@ -39,7 +39,7 @@
         shares = outputs[:, :HORIZON]
         bound = outputs[:, HORIZON:]
         partial_load = jnp.dot(onehot.T, shares, precision=lax.Precision.HIGHEST)
-        floor_load = lax.psum(partial_load, "zone")
+        floor_load = jnp.sum(lax.all_gather(partial_load, "zone"), axis=0)
         total = lax.psum(floor_load, "floor")
         excess = (total - demand) * (LOOPS / zones_all)
         shift = jnp.dot(onehot, excess + price, precision=lax.Precision.HIGHEST)

time: 92.1 us -> 86.8 us (0.942)
  blocking collectives: 78.3 us -> 73.1 us
    psum x2 -> x0, blocking collectives: 30.8 us -> none  [local(): floor_load = lax.psum(partial_load, 'zone')]
    all_gather x0 -> x2, blocking collectives: none -> 25.5 us  [local(): floor_load = jnp.sum(lax.all_gather(partial_load, 'zone'), axis=0)]
where the time goes in v1:
time: 86.8 us; the launch traced here: 86.6 us
  blocking collectives  73.1 us (84%)
  matrix products  11.7 us (13%)
  other arithmetic  0.91 us (1%)
    all_gather x2, blocking collectives, local(): floor_bound = lax.all_gather(bound, 'zone', axis=0, tiled=True)  29.7 us
    all_gather x2, blocking collectives, local(): floor_load = jnp.sum(lax.all_gather(partial_load, 'zone'), axis=0)  25.5 us
    psum x2, blocking collectives, local(): total = lax.psum(floor_load, 'floor')  17.9 us
    dot_general x2, matrix products, local(): jnp.einsum('zkv,zv->zk', plant_map, control, precision=lax.Precision.HIGH...  7 us
    dot_general x2, matrix products, local(): jnp.einsum('zkv,zk->zv', factor, target, precision=lax.Precision.HIGHEST)  2.88 us

profile of v1, /device:TPU:0, one launch (start us, length us, event | category | flops | bytes accessed | tf_op | source)
XLA Modules:
  0.0 86.6 jit_solution(2132968364415672605)
XLA Ops:
  0.6 0.0 copy-start
  0.7 4.4 %fusion.5 = f32[16,1,96]{2,1,0:T(1,128)S(1)} fusion(f32[16,96,384]{2,1,0:T(8,128)} %param.10, f32[16,384,1]{1,0,2:T(8,128)} %bitcast.47), kind=kOutput, calls=%fused_computation.13 | convolution fusion | flops 7077888 | bytes 2390016 | tf_op jit(solution)/shard_map/zkv,zv->zk/dot_general | solution.py:38
  5.1 0.1 slice.17
  5.2 15.7 %all_gather.20 = f32[128,48]{1,0:T(8,128)S(1)} all-gather(f32[16,48]{1,0:T(8,128)S(1)} %slice.17), channel_id=1, replica_groups=mesh['floor'=4,'zone'=8] {'zone'}, dimensions={0}, use_global_device_ids=true | all-gather | bytes 27648 | tf_op jit(solution)/shard_map/all_gather | solution.py:48
  20.9 0.1 convert_reduce_fusion
  21.0 0.2 multiply_subtract_fusion.1
  21.1 0.0 copy-done.8
  21.1 0.3 convolution_bitcast_fusion.1
  21.4 12.8 %all-gather.2 = f32[8,4,48]{2,1,0:T(4,128)S(1)} all-gather(f32[1,4,48]{2,1,0:T(4,128)S(1)} %convolution_bitcast_fusion.1), channel_id=2, replica_groups=mesh['floor'=4,'zone'=8] {'zone'}, dimensions={0}, use_global_device_ids=true | all-gather | bytes 6912 | tf_op jit(solution)/shard_map/all_gather | solution.py:42
  34.2 9.9 %psum.14 = f32[4,48]{1,0:T(4,128)S(1)} all-reduce(f32[4,48]{1,0:T(4,128)S(1)} %reduce_sum.27), channel_id=1, replica_groups=mesh['floor'=4,'zone'=8] {'floor'}, use_global_device_ids=true, to_apply=%region_1.0 | all-reduce | flops 192 | bytes 1536 | tf_op jit(solution)/shard_map/psum | solution.py:43
  44.1 0.2 convolution_subtract_fusion.1
  44.3 0.1 pad_maximum_fusion
  44.4 1.4 %fusion.22 = f32[16,1,384]{2,1,0:T(1,128)S(1)} fusion(f32[16,96,1]{1,2,0:T(1,128)S(1)} %bitcast.45, f32[16,96,384]{2,1,0:T(8,128)S(1)} %copy-done), kind=kOutput, calls=%fused_computation.39 | convolution fusion | flops 7077888 | bytes 2390016 | tf_op jit(solution)/shard_map/zkv,zk->zv/dot_general | solution.py:55
  45.9 2.6 %fusion.3 = f32[16,1,96]{2,1,0:T(1,128)S(1)} fusion(f32[16,96,384]{2,1,0:T(8,128)S(1)} %copy-done.1, f32[16,384,1]{1,0,2:T(8,128)S(1)} %fusion.2), kind=kOutput, calls=%fused_computation.11 | convolution fusion | flops 7077888 | bytes 2390016 | tf_op jit(solution)/shard_map/zkv,zv->zk/dot_general | solution.py:38
  48.4 0.1 slice.19
  48.5 14.0 %all_gather.23 = f32[128,48]{1,0:T(8,128)S(1)} all-gather(f32[16,48]{1,0:T(8,128)S(1)} %slice.19), channel_id=1, replica_groups=mesh['floor'=4,'zone'=8] {'zone'}, dimensions={0}, use_global_device_ids=true | all-gather | bytes 27648 | tf_op jit(solution)/shard_map/all_gather | solution.py:48
  62.5 0.8 multiply_add_fusion
  63.3 0.3 convolution_bitcast_fusion
  63.5 12.8 %all-gather.3 = f32[8,4,48]{2,1,0:T(4,128)S(1)} all-gather(f32[1,4,48]{2,1,0:T(4,128)S(1)} %convolution_bitcast_fusion), channel_id=3, replica_groups=mesh['floor'=4,'zone'=8] {'zone'}, dimensions={0}, use_global_device_ids=true | all-gather | bytes 6912 | tf_op jit(solution)/shard_map/all_gather | solution.py:42
  76.3 8.0 %psum.15 = f32[4,48]{1,0:T(4,128)S(1)} all-reduce(f32[4,48]{1,0:T(4,128)S(1)} %reduce_sum.33), channel_id=1, replica_groups=mesh['floor'=4,'zone'=8] {'floor'}, use_global_device_ids=true, to_apply=%region_4.0 | all-reduce | flops 192 | bytes 1536 | tf_op jit(solution)/shard_map/psum | solution.py:43
  84.3 0.2 convolution_subtract_fusion
  84.5 0.1 pad_maximum_fusion.1
  84.6 1.4 %fusion.23 = f32[16,1,384]{2,1,0:T(1,128)S(1)} fusion(f32[16,96,1]{1,2,0:T(1,128)S(1)} %bitcast.46, f32[16,96,384]{2,1,0:T(8,128)S(1)} %copy-done), kind=kOutput, calls=%fused_computation.40 | convolution fusion | flops 7077888 | bytes 2390016 | tf_op jit(solution)/shard_map/zkv,zk->zv/dot_general | solution.py:55
  86.0 0.6 fusion
  (20 shorter events, 0.1 us)
Async XLA Ops:
  0.6 43.7 %copy-start = (f32[16,96,384]{2,1,0:T(8,128)S(1)}, f32[16,96,384]{2,1,0:T(8,128)}, u32[]{:S(2)}) copy-start(f32[16,96,384]{2,1,0:T(8,128)} %param.9) | copy-start | bytes 7077892
  0.6 20.3 %copy-start.3 = (f32[16,48]{1,0:T(8,128)S(1)}, f32[16,48]{1,0:T(8,128)}, u32[]{:S(2)}) copy-start(f32[16,48]{1,0:T(8,128)} %param.15) | copy-start | bytes 9220
  0.7 20.2 %copy-start.4 = (s32[16,4]{0,1:T(4,128)S(1)}, s32[16,4]{0,1:T(4,128)}, u32[]{:S(2)}) copy-start(s32[16,4]{0,1:T(4,128)} %param.16) | copy-start | bytes 772
  0.7 20.5 %copy-start.8 = (s32[16]{0:T(128)S(1)}, s32[16]{0:T(128)}, u32[]{:S(2)}) copy-start(s32[16]{0:T(128)} %param.17) | copy-start | bytes 196
  0.7 43.4 %copy-start.5 = (f32[4,48]{1,0:T(4,128)S(1)}, f32[4,48]{1,0:T(4,128)}, u32[]{:S(2)}) copy-start(f32[4,48]{1,0:T(4,128)} %param.14) | copy-start | bytes 2308
  0.7 43.4 %copy-start.6 = (f32[4,48]{1,0:T(4,128)S(1)}, f32[4,48]{1,0:T(4,128)}, u32[]{:S(2)}) copy-start(f32[4,48]{1,0:T(4,128)} %param.13) | copy-start | bytes 2308
  0.7 45.1 %copy-start.2 = (f32[16,384]{1,0:T(8,128)S(1)}, f32[16,384]{1,0:T(8,128)}, u32[]{:S(2)}) copy-start(f32[16,384]{1,0:T(8,128)} %param.11) | copy-start | bytes 73732
  44.1 1.7 %copy-start.1 = (f32[16,96,384]{2,1,0:T(8,128)S(1)}, f32[16,96,384]{2,1,0:T(8,128)}, u32[]{:S(2)}) copy-start(f32[16,96,384]{2,1,0:T(8,128)} %param.10) | copy-start | bytes 7077892
  84.3 2.3 %copy-start.7 = (f32[4,48]{1,0:T(4,128)}, f32[4,48]{1,0:T(4,128)S(1)}, u32[]{:S(2)}) copy-start(f32[4,48]{1,0:T(4,128)S(1)} %multiply_add_fusion.2) | copy-start | bytes 2308
